TPU v7x, 128 devices: a whole 4x4x4 slice. The times are simulated.
128 devices in a mesh: grp: 4 (over y), tile: 32 (over x, z, core).
Axes of the slice: x: 4, y: 4, z: 4, core: 2. Of those that a mesh axis runs over, the one named last changes fastest.
Arguments:
- base_rhs: float32 [1024, 16384], P('grp', 'tile'), may hold values from -6 to 6
- depth: float32 [1024, 16384], P('grp', 'tile'), may hold values from 0.25 to 2
- ssh_prev: float32 [1024, 16384], P('grp', 'tile'), may hold values from -6 to 6
- currents: float32 [2, 1024, 16384], P(None, 'grp', 'tile'), may hold values from -3 to 3
- land_blocks: int32 [128, 2048], P('grp', 'tile'), may hold values 0 or 1
- ice_thick: float32 [2, 256, 16384], P(None, 'grp', 'tile'), may hold values from 0.25 to 4
- ice_blocks: int32 [2, 32, 2048], P(None, 'grp', 'tile'), may hold values 0 or 1
- ice_vel: float32 [2, 2, 256, 16384], P(None, None, 'grp', 'tile'), may hold values from -3 to 3
- ice_stress: float32 [3, 2, 256, 16384], P(None, None, 'grp', 'tile'), may hold values from -5 to 5
- wind: float32 [2, 2, 256, 16384], P(None, None, 'grp', 'tile'), may hold values from -6 to 6
Outputs:
- ssh: float32 [1024, 16384], P('grp', 'tile')
- ice_vel_out: float32 [2, 2, 256, 16384], P(None, None, 'grp', 'tile')
- ice_stress_out: float32 [3, 2, 256, 16384], P(None, None, 'grp', 'tile')
All inputs are finite; a program needn't handle non-finite values. No bound on the sum of `land_blocks` or of `ice_blocks` on one device may be relied on, other than what follows from the above.
Results may differ from a plain program's by a relative error of at most 0.0001.
Values sent between devices are 32-bit elements; how exact they have to be, the bound alone decides.
A program may use at most 64 MiB of HBM per device.

v0:
```python
import jax
import jax.numpy as jnp
from jax import lax
from jax.sharding import Mesh
from jax.sharding import PartitionSpec as P

BS = 8
NSUB = 8
ITERS = 3
GRP_TILE = ("grp", "tile_0", "tile_1", "tile_2")
TILE = ("tile_0", "tile_1", "tile_2")
DAMP = 0.05
RELAX = 0.2
STRENGTH = 0.5
DRAG = 1.0
STEP = 0.5


def with_halo(array, sides, width):
    edges = {}
    for axis, dim in sides:
        devices, length = (lax.axis_size(axis), array.shape[dim])
        up = [(i, (i + 1) % devices) for i in range(devices - 1)]
        last = lax.slice_in_dim(array, length - width, length, axis=dim)
        first = lax.slice_in_dim(array, 0, width, axis=dim)
        edges[dim] = (
            lax.ppermute(last, axis, up),
            lax.ppermute(first, axis, [(b, a) for a, b in up]),
        )
    done = []
    for _, dim in sides:
        low, high = edges[dim]
        around = [(width, width) if d in done else (0, 0) for d in range(array.ndim)]
        array = jnp.concatenate([jnp.pad(low, around), array, jnp.pad(high, around)], axis=dim)
        done.append(dim)
    return array


def by_axis(array, axes):
    for axis in axes:
        array = lax.psum(array, axis)
    return array


def extended(array, sides, width):
    for axis, dim in sides:
        devices, length = (lax.axis_size(axis), array.shape[dim])
        up = [(i, (i + 1) % devices) for i in range(devices - 1)]
        down = [(j, i) for i, j in up]
        last = lax.slice_in_dim(array, length - width, length, axis=dim)
        first = lax.slice_in_dim(array, 0, width, axis=dim)
        before = lax.ppermute(last, axis, up)
        after = lax.ppermute(first, axis, down)
        array = jnp.concatenate([before, array, after], axis=dim)
    return array


def strain_rates(u_pad, v_pad):
    du_dx = u_pad[..., 1:, :-1] - u_pad[..., :-1, :-1]
    du_dy = u_pad[..., :-1, 1:] - u_pad[..., :-1, :-1]
    dv_dx = v_pad[..., 1:, :-1] - v_pad[..., :-1, :-1]
    dv_dy = v_pad[..., :-1, 1:] - v_pad[..., :-1, :-1]
    return (du_dx + dv_dy, du_dx - dv_dy, du_dy + dv_dx)


def relax_stress(previous, strength, div_rate, tens_rate, shear_rate):
    deformation = jnp.sqrt(
        div_rate * div_rate + tens_rate * tens_rate + shear_rate * shear_rate + 1.0
    )
    relax_scale = 1.0 / (1.0 + RELAX)
    div_part = (previous[0] + RELAX * strength * (div_rate / deformation - 1.0)) * relax_scale
    tens_part = (previous[1] + RELAX * strength * tens_rate / deformation) * relax_scale
    shear_part = (previous[2] + RELAX * strength * shear_rate / deformation) * relax_scale
    return jnp.stack([div_part, tens_part, shear_part])


def along_rows(field):
    return field[..., 1:, 1:] - field[..., :-1, 1:]


def along_cols(field):
    return field[..., 1:, 1:] - field[..., 1:, :-1]


def stress_force(stress_pad):
    force_x = 0.5 * along_rows(stress_pad[0] + stress_pad[1]) + along_cols(stress_pad[2])
    force_y = 0.5 * along_cols(stress_pad[0] - stress_pad[1]) + along_rows(stress_pad[2])
    return jnp.stack([force_x, force_y])


def momentum(velocity, force, ice_mass, ice_cover, wind, ocean_flow):
    return (
        ice_cover
        * (ice_mass * velocity + STEP * (force + wind + DRAG * ocean_flow))
        / (ice_mass + STEP * DRAG)
    )


def face_weights(depth_pad):
    centre = depth_pad[1:-1, 1:-1]
    return (
        centre * depth_pad[2:, 1:-1],
        centre * depth_pad[:-2, 1:-1],
        centre * depth_pad[1:-1, 2:],
        centre * depth_pad[1:-1, :-2],
    )


def apply_operator(field_pad, weights):
    field = field_pad[1:-1, 1:-1]
    north_weight, south_weight, east_weight, west_weight = weights
    return (
        DAMP * field
        + north_weight * (field - field_pad[2:, 1:-1])
        + south_weight * (field - field_pad[:-2, 1:-1])
        + east_weight * (field - field_pad[1:-1, 2:])
        + west_weight * (field - field_pad[1:-1, :-2])
    )


def expand(blocks):
    return jnp.repeat(jnp.repeat(blocks, BS, axis=-2), BS, axis=-1).astype(jnp.float32)


def operate(field, weights):
    field_pad = with_halo(field, (("grp", 0), (TILE, 1)), 1)
    return apply_operator(field_pad, weights)


def pair_sums(residual, precond, applied):
    return (
        by_axis(jnp.sum(residual * precond), GRP_TILE),
        by_axis(jnp.sum(precond * applied), GRP_TILE),
    )


def local_subcycle(velocity, stress, strength, ice_mass, ice_cover, wind, ocean_flow):
    vel_pad = jnp.pad(velocity, ((0, 0), (0, 0), (1, 1), (1, 1)))
    strain = strain_rates(vel_pad[0], vel_pad[1])
    stress = relax_stress(
        stress, strength, strain[0][:, 1:, 1:], strain[1][:, 1:, 1:], strain[2][:, 1:, 1:]
    )
    stress_pad = jnp.pad(stress, ((0, 0), (0, 0), (1, 0), (1, 0)))
    velocity = momentum(velocity, stress_force(stress_pad), ice_mass, ice_cover, wind, ocean_flow)
    return (velocity, stress)


def shards(
    base_rhs,
    depth,
    ssh_prev,
    currents,
    land_blocks,
    ice_thick,
    ice_blocks,
    ice_vel,
    ice_stress,
    wind,
):
    groups = lax.axis_size("grp")
    grp_index = lax.axis_index("grp")
    ocean_cols = base_rhs.shape[1]
    ice_rows = ice_thick.shape[1]
    cap_rows = ice_rows * groups
    wet_cells = expand(land_blocks)
    ice_cover = expand(ice_blocks)
    at_north = (grp_index == 0).astype(jnp.float32)
    at_south = (grp_index == groups - 1).astype(jnp.float32)
    outgoing = jnp.stack([currents * at_north, currents * at_south], axis=1)
    outgoing = outgoing.reshape(2, 2, groups, ice_rows, ocean_cols)
    incoming = lax.all_to_all(outgoing, "grp", split_axis=2, concat_axis=2, tiled=True)
    ocean_flow = jnp.sum(incoming, axis=2)
    strength = STRENGTH * ice_thick * ice_cover
    ice_mass = ice_thick * ice_cover + 1.0
    velocity = ice_vel
    stress = ice_stress
    bundle = jnp.concatenate(
        [velocity, stress, wind, ocean_flow, strength[None], ice_mass[None], ice_cover[None]],
        axis=0,
    )
    widened = extended(bundle, (("grp", 2), (TILE, 3)), NSUB)
    wide_vel = widened[0:2]
    wide_stress = widened[2:5]
    wide_wind = widened[5:7]
    wide_flow = widened[7:9]
    wide_strength = widened[9]
    wide_mass = widened[10]
    wide_cover = widened[11]
    for subcycle in range(NSUB):
        wide_vel, wide_stress = local_subcycle(
            wide_vel, wide_stress, wide_strength, wide_mass, wide_cover, wide_wind, wide_flow
        )
    velocity = wide_vel[:, :, NSUB : NSUB + ice_rows, NSUB : NSUB + ocean_cols]
    stress = wide_stress[:, :, NSUB : NSUB + ice_rows, NSUB : NSUB + ocean_cols]
    ice_drag = DRAG * ice_cover * (velocity - ocean_flow)
    empty_slot = jnp.zeros_like(ice_drag[:, 0])
    parcel = jnp.stack([ice_drag[:, 0]] + [empty_slot] * (groups - 2) + [ice_drag[:, 1]], axis=1)
    returned = lax.all_to_all(parcel, "grp", split_axis=1, concat_axis=1, tiled=True).reshape(
        2, cap_rows, ocean_cols
    )
    ocean_drag = jnp.where(
        grp_index == 0, returned, jnp.where(grp_index == groups - 1, returned, 0.0)
    )
    forcing_pad = with_halo(
        jnp.stack([ocean_drag[0], ocean_drag[1], depth * wet_cells]), (("grp", 1), (TILE, 2)), 1
    )
    spread = (
        forcing_pad[0, 1:-1, 1:-1]
        - forcing_pad[0, :-2, 1:-1]
        + (forcing_pad[1, 1:-1, 1:-1] - forcing_pad[1, 1:-1, :-2])
    )
    forcing = wet_cells * (base_rhs + spread)
    weights = face_weights(forcing_pad[2])
    diagonal = DAMP + weights[0] + weights[1] + weights[2] + weights[3]
    solution = ssh_prev
    residual = forcing - operate(solution, weights)
    precond = residual / diagonal
    applied = operate(precond, weights)
    precond_norm, curvature_sum = pair_sums(residual, precond, applied)
    step_size = precond_norm / curvature_sum
    direction = precond
    search_image = applied
    for iteration in range(ITERS):
        solution = solution + step_size * direction
        residual = residual - step_size * search_image
        if iteration + 1 < ITERS:
            precond = residual / diagonal
            applied = operate(precond, weights)
            norm_next, curvature_sum = pair_sums(residual, precond, applied)
            beta_ratio = norm_next / precond_norm
            step_size = norm_next / (curvature_sum - beta_ratio * norm_next / step_size)
            direction = precond + beta_ratio * direction
            search_image = applied + beta_ratio * search_image
            precond_norm = norm_next
    return (solution, velocity, stress)


def solution(mesh):
    finer = Mesh(
        mesh.devices.reshape(mesh.shape["grp"], 4, 4, 2), ("grp", "tile_0", "tile_1", "tile_2")
    )
    return jax.shard_map(
        shards,
        mesh=finer,
        in_specs=(
            P("grp", TILE),
            P("grp", TILE),
            P("grp", TILE),
            P(None, "grp", TILE),
            P("grp", TILE),
            P(None, "grp", TILE),
            P(None, "grp", TILE),
            P(None, None, "grp", TILE),
            P(None, None, "grp", TILE),
            P(None, None, "grp", TILE),
        ),
        out_specs=(P("grp", TILE), P(None, None, "grp", TILE), P(None, None, "grp", TILE)),
        check_vma=False,
    )
```

profile of v0, /device:TPU:1, one launch (start us, length us, event | category | flops | bytes accessed | tf_op | source)
XLA Modules:
  0.0 336.6 jit_solution(16348324338508460184)
XLA Ops:
  3.9 5.1 %all-to-all-start = ((f32[2,2,4,64,512]{4,3,0,1,2:T(8,128)}), f32[2,2,4,64,512]{4,3,0,1,2:T(8,128)}, u32[]{:S(2)}, u32[]{:S(2)}) async-start(f32[2,2,4,64,512]{4,3,0,1,2:T(8,128)} %copy.115), calls=%async_computation | async-start | bytes 4194304 | tf_op jit(solution)/shard_map/all_to_all | solution.py:171
  12.7 22.3 %all-to-all-done = f32[2,2,4,64,512]{4,3,0,1,2:T(8,128)} async-done(((f32[2,2,4,64,512]{4,3,0,1,2:T(8,128)}), f32[2,2,4,64,512]{4,3,0,1,2:T(8,128)}, u32[]{:S(2)}, u32[]{:S(2)}) %all-to-all-start) | async-done | bytes 2097184 | tf_op jit(solution)/shard_map/all_to_all | solution.py:171
  35.0 2.7 reduce_sum.63
  40.0 2.4 collective-permute-start
  43.7 5.6 %collective-permute-done = f32[12,2,8,512]{3,2,1,0:T(8,128)S(1)} collective-permute-done((f32[12,2,8,512]{3,2,1,0:T(8,128)S(1)}, f32[12,2,8,512]{3,2,1,0:T(8,128)S(1)}, u32[]{:S(2)}, u32[]{:S(2)}) %collective-permute-start) | collective-permute-done | bytes 393248 | tf_op jit(solution)/shard_map/ppermute | solution.py:52
  49.3 3.9 %collective-permute-done.1 = f32[12,2,8,512]{3,2,1,0:T(8,128)S(1)} collective-permute-done((f32[12,2,8,512]{3,2,1,0:T(8,128)S(1)}, f32[12,2,8,512]{3,2,1,0:T(8,128)S(1)}, u32[]{:S(2)}, u32[]{:S(2)}) %collective-permute-start.1) | collective-permute-done | bytes 393248 | tf_op jit(solution)/shard_map/ppermute | solution.py:53
  53.9 1.6 pad_maximum_fusion.6
  55.6 2.1 copy.121
  57.7 6.1 %collective-permute-start.2 = (f32[12,2,80,8]{2,3,1,0:T(8,128)}, f32[12,2,80,8]{2,3,1,0:T(8,128)}, u32[]{:S(2)}, u32[]{:S(2)}) collective-permute-start(f32[12,2,80,8]{2,3,1,0:T(8,128)} %copy.121), channel_id=1, source_target_pairs={{0,1},{1,2},{2,3},{3,4},{4,5},{5,6},{6,7},{7,8},{8,9},{9,10},{10,1... | collective-permute-start | bytes 184328 | tf_op jit(solution)/shard_map/ppermute | solution.py:52
  63.8 2.1 copy.122
  65.9 1.9 collective-permute-start.3
  67.9 2.2 copy.123
  70.1 2.1 collective-permute-done.3
  72.1 2.2 copy.124
  74.3 4.6 %pad_maximum_fusion = f32[12,2,80,528]{3,2,1,0:T(8,128)S(1)} fusion(f32[12,2,80,8]{3,2,1,0:T(8,128)} %copy.124, f32[12,2,8,512]{3,2,1,0:T(8,128)} %copy-done.2, f32[12,2,64,512]{3,2,1,0:T(8,128)S(1)} %constant_dynamic-update-slice_fusion, f32[12,2,8,512]{3,2,1,0:T(8,128)S(1)} %collective-permute-done, f32[12,2,80,8]{3,2,1,0:T(8,128)} %copy.123), kind=kLoop, calls=%fused_computation | loop fusion | flops 4055040 | bytes 8110080 | tf_op jit(solution)/shard_map/concatenate | solution.py:54
  112.5 3.6 %all-to-all-start.1 = ((f32[2,4,64,512]{3,2,0,1:T(8,128)}), f32[2,4,64,512]{3,2,0,1:T(8,128)S(1)}, u32[]{:S(2)}, u32[]{:S(2)}) async-start(f32[2,4,64,512]{3,2,0,1:T(8,128)} %pad_maximum_fusion.3), calls=%async_computation.1 | async-start | bytes 2097152 | tf_op jit(solution)/shard_map/all_to_all | solution.py:198
  116.3 1.9 collective-permute-start.10
  118.4 2.0 copy.138
  121.5 7.6 %all-to-all-done.1 = f32[2,4,64,512]{3,2,0,1:T(8,128)S(1)} async-done(((f32[2,4,64,512]{3,2,0,1:T(8,128)}), f32[2,4,64,512]{3,2,0,1:T(8,128)S(1)}, u32[]{:S(2)}, u32[]{:S(2)}) %all-to-all-start.1) | async-done | bytes 1048608 | tf_op jit(solution)/shard_map/all_to_all | solution.py:198
  130.3 2.5 copy.137
  137.0 2.2 collective-permute-start.4
  141.9 4.4 %collective-permute-start.5 = (f32[3,256,1]{1,2,0:T(1,128)S(1)}, f32[3,256,1]{1,2,0:T(1,128)S(1)}, u32[]{:S(2)}, u32[]{:S(2)}) collective-permute-start(f32[3,256,1]{1,2,0:T(1,128)S(1)} %get-tuple-element.96), channel_id=1, source_target_pairs={{0,1},{1,2},{2,3},{3,4},{4,5},{5,6},{6,7},{7,8},{8,9},{9,10},{10,1... | collective-permute-start | bytes 9224 | tf_op jit(solution)/shard_map/ppermute | solution.py:27
  146.2 1.9 collective-permute-start.7
  151.6 3.6 %collective-permute-start.11 = (f32[256,1]{0,1:T(1,128)S(1)}, f32[256,1]{0,1:T(1,128)S(1)}, u32[]{:S(2)}, u32[]{:S(2)}) collective-permute-start(f32[256,1]{0,1:T(1,128)S(1)} %get-tuple-element.170), channel_id=1, source_target_pairs={{0,1},{1,2},{2,3},{3,4},{4,5},{5,6},{6,7},{7,8},{8,9},{9,10},{10,1... | collective-permute-start | bytes 3080 | tf_op jit(solution)/shard_map/ppermute | solution.py:27
  157.9 5.6 %collective-permute-start.9 = (f32[1,512]{0,1:T(8,128)}, f32[1,512]{0,1:T(8,128)}, u32[]{:S(2)}, u32[]{:S(2)}) collective-permute-start(f32[1,512]{0,1:T(8,128)} %copy.149), channel_id=1, source_target_pairs={{0,32},{32,64},{64,96},{1,33},{33,65},{65,97},{2,34},{34,66},{66,9... | collective-permute-start | bytes 6152 | tf_op jit(solution)/shard_map/ppermute | solution.py:27
  168.4 3.4 fusion.196
  173.2 4.5 %collective-permute-start.13 = (f32[1,512]{0,1:T(8,128)S(1)}, f32[1,512]{0,1:T(8,128)S(1)}, u32[]{:S(2)}, u32[]{:S(2)}) collective-permute-start(f32[1,512]{0,1:T(8,128)S(1)} %get-tuple-element.165), channel_id=1, source_target_pairs={{0,32},{32,64},{64,96},{1,33},{33,65},{65,97},{2,34},{34,66},{66,9... | collective-permute-start | bytes 6152 | tf_op jit(solution)/shard_map/ppermute | solution.py:27
  177.7 2.1 collective-permute-start.14
  179.8 3.7 %collective-permute-start.15 = (f32[256,1]{0,1:T(1,128)S(1)}, f32[256,1]{0,1:T(1,128)S(1)}, u32[]{:S(2)}, u32[]{:S(2)}) collective-permute-start(f32[256,1]{0,1:T(1,128)S(1)} %get-tuple-element.164), channel_id=1, source_target_pairs={{0,1},{1,2},{2,3},{3,4},{4,5},{5,6},{6,7},{7,8},{8,9},{9,10},{10,1... | collective-permute-start | bytes 3080 | tf_op jit(solution)/shard_map/ppermute | solution.py:27
  185.6 9.8 %all-reduce.34 = (f32[]{:T(128)}, f32[]{:T(128)}) all-reduce(f32[]{:T(128)} %get-tuple-element.20, f32[]{:T(128)} %get-tuple-element.19), channel_id=1, replica_groups=mesh['grp'=4,'tile_0'=4,'tile_1'=4,'tile_2'=2] {'grp'}, use_global_device_ids=true, to_apply=%region_2.3 | all-reduce | flops 2 | bytes 16 | tf_op jit(solution)/shard_map/psum | solution.py:41
  195.4 10.2 %all-reduce.31 = (f32[]{:T(128)}, f32[]{:T(128)}) all-reduce(f32[]{:T(128)} %get-tuple-element.37, f32[]{:T(128)} %get-tuple-element.38), channel_id=1, replica_groups=mesh['grp'=4,'tile_0'=4,'tile_1'=4,'tile_2'=2] {'tile_0'}, use_global_device_ids=true, to_apply=%region_3.4 | all-reduce | flops 2 | bytes 16 | tf_op jit(solution)/shard_map/psum | solution.py:41
  205.6 9.1 %all-reduce.28 = (f32[]{:T(128)}, f32[]{:T(128)}) all-reduce(f32[]{:T(128)} %get-tuple-element.31, f32[]{:T(128)} %get-tuple-element.32), channel_id=1, replica_groups=mesh['grp'=4,'tile_0'=4,'tile_1'=4,'tile_2'=2] {'tile_1'}, use_global_device_ids=true, to_apply=%region_4.5 | all-reduce | flops 2 | bytes 16 | tf_op jit(solution)/shard_map/psum | solution.py:41
  214.7 10.6 %all-reduce.37 = (f32[]{:T(128)}, f32[]{:T(128)}) all-reduce(f32[]{:T(128)} %get-tuple-element.25, f32[]{:T(128)} %get-tuple-element.26), channel_id=1, replica_groups=mesh['grp'=4,'tile_0'=4,'tile_1'=4,'tile_2'=2] {'tile_2'}, use_global_device_ids=true, to_apply=%region_5.6 | all-reduce | flops 2 | bytes 16 | tf_op jit(solution)/shard_map/psum | solution.py:41
  229.3 4.0 %collective-permute-start.17 = (f32[1,512]{0,1:T(8,128)S(1)}, f32[1,512]{0,1:T(8,128)S(1)}, u32[]{:S(2)}, u32[]{:S(2)}) collective-permute-start(f32[1,512]{0,1:T(8,128)S(1)} %get-tuple-element.161), channel_id=1, source_target_pairs={{0,32},{32,64},{64,96},{1,33},{33,65},{65,97},{2,34},{34,66},{66,9... | collective-permute-start | bytes 6152 | tf_op jit(solution)/shard_map/ppermute | solution.py:27
  233.3 2.8 collective-permute-start.18
  236.1 3.5 %collective-permute-start.19 = (f32[256,1]{0,1:T(1,128)S(1)}, f32[256,1]{0,1:T(1,128)S(1)}, u32[]{:S(2)}, u32[]{:S(2)}) collective-permute-start(f32[256,1]{0,1:T(1,128)S(1)} %get-tuple-element.160), channel_id=1, source_target_pairs={{0,1},{1,2},{2,3},{3,4},{4,5},{5,6},{6,7},{7,8},{8,9},{9,10},{10,1... | collective-permute-start | bytes 3080 | tf_op jit(solution)/shard_map/ppermute | solution.py:27
  240.4 2.1 multiply_reduce_fusion.1
  242.5 7.5 %all-reduce.33 = (f32[]{:T(128)}, f32[]{:T(128)}) all-reduce(f32[]{:T(128)} %get-tuple-element.18, f32[]{:T(128)} %get-tuple-element.17), channel_id=1, replica_groups=mesh['grp'=4,'tile_0'=4,'tile_1'=4,'tile_2'=2] {'grp'}, use_global_device_ids=true, to_apply=%region_12.13 | all-reduce | flops 2 | bytes 16 | tf_op jit(solution)/shard_map/psum | solution.py:41
  250.0 7.4 %all-reduce.30 = (f32[]{:T(128)}, f32[]{:T(128)}) all-reduce(f32[]{:T(128)} %get-tuple-element.35, f32[]{:T(128)} %get-tuple-element.36), channel_id=1, replica_groups=mesh['grp'=4,'tile_0'=4,'tile_1'=4,'tile_2'=2] {'tile_0'}, use_global_device_ids=true, to_apply=%region_13.14 | all-reduce | flops 2 | bytes 16 | tf_op jit(solution)/shard_map/psum | solution.py:41
  257.4 9.2 %all-reduce.27 = (f32[]{:T(128)}, f32[]{:T(128)}) all-reduce(f32[]{:T(128)} %get-tuple-element.29, f32[]{:T(128)} %get-tuple-element.30), channel_id=1, replica_groups=mesh['grp'=4,'tile_0'=4,'tile_1'=4,'tile_2'=2] {'tile_1'}, use_global_device_ids=true, to_apply=%region_14.15 | all-reduce | flops 2 | bytes 16 | tf_op jit(solution)/shard_map/psum | solution.py:41
  266.6 10.5 %all-reduce.36 = (f32[]{:T(128)}, f32[]{:T(128)}) all-reduce(f32[]{:T(128)} %get-tuple-element.23, f32[]{:T(128)} %get-tuple-element.24), channel_id=1, replica_groups=mesh['grp'=4,'tile_0'=4,'tile_1'=4,'tile_2'=2] {'tile_2'}, use_global_device_ids=true, to_apply=%region_15.16 | all-reduce | flops 2 | bytes 16 | tf_op jit(solution)/shard_map/psum | solution.py:41
  284.6 4.0 %collective-permute-start.21 = (f32[1,512]{0,1:T(8,128)S(1)}, f32[1,512]{0,1:T(8,128)S(1)}, u32[]{:S(2)}, u32[]{:S(2)}) collective-permute-start(f32[1,512]{0,1:T(8,128)S(1)} %get-tuple-element.157), channel_id=1, source_target_pairs={{0,32},{32,64},{64,96},{1,33},{33,65},{65,97},{2,34},{34,66},{66,9... | collective-permute-start | bytes 6152 | tf_op jit(solution)/shard_map/ppermute | solution.py:27
  288.6 2.8 collective-permute-start.22
  291.4 3.5 %collective-permute-start.23 = (f32[256,1]{0,1:T(1,128)S(1)}, f32[256,1]{0,1:T(1,128)S(1)}, u32[]{:S(2)}, u32[]{:S(2)}) collective-permute-start(f32[256,1]{0,1:T(1,128)S(1)} %get-tuple-element.156), channel_id=1, source_target_pairs={{0,1},{1,2},{2,3},{3,4},{4,5},{5,6},{6,7},{7,8},{8,9},{9,10},{10,1... | collective-permute-start | bytes 3080 | tf_op jit(solution)/shard_map/ppermute | solution.py:27
  298.3 7.2 %all-reduce.32 = (f32[]{:T(128)}, f32[]{:T(128)}) all-reduce(f32[]{:T(128)} %get-tuple-element.16, f32[]{:T(128)} %get-tuple-element.15), channel_id=1, replica_groups=mesh['grp'=4,'tile_0'=4,'tile_1'=4,'tile_2'=2] {'grp'}, use_global_device_ids=true, to_apply=%region_22.23 | all-reduce | flops 2 | bytes 16 | tf_op jit(solution)/shard_map/psum | solution.py:41
  305.5 6.7 %all-reduce.29 = (f32[]{:T(128)}, f32[]{:T(128)}) all-reduce(f32[]{:T(128)} %get-tuple-element.33, f32[]{:T(128)} %get-tuple-element.34), channel_id=1, replica_groups=mesh['grp'=4,'tile_0'=4,'tile_1'=4,'tile_2'=2] {'tile_0'}, use_global_device_ids=true, to_apply=%region_23.24 | all-reduce | flops 2 | bytes 16 | tf_op jit(solution)/shard_map/psum | solution.py:41
  312.2 9.8 %all-reduce.26 = (f32[]{:T(128)}, f32[]{:T(128)}) all-reduce(f32[]{:T(128)} %get-tuple-element.27, f32[]{:T(128)} %get-tuple-element.28), channel_id=1, replica_groups=mesh['grp'=4,'tile_0'=4,'tile_1'=4,'tile_2'=2] {'tile_1'}, use_global_device_ids=true, to_apply=%region_24.25 | all-reduce | flops 2 | bytes 16 | tf_op jit(solution)/shard_map/psum | solution.py:41
  322.0 9.2 %all-reduce.35 = (f32[]{:T(128)}, f32[]{:T(128)}) all-reduce(f32[]{:T(128)} %get-tuple-element.21, f32[]{:T(128)} %get-tuple-element.22), channel_id=1, replica_groups=mesh['grp'=4,'tile_0'=4,'tile_1'=4,'tile_2'=2] {'tile_2'}, use_global_device_ids=true, to_apply=%region_25.26 | all-reduce | flops 2 | bytes 16 | tf_op jit(solution)/shard_map/psum | solution.py:41
  (230 shorter events, 78.9 us)
Async XLA Ops:
  3.9 5.1 %copy-start.35 = (s32[2,8,64]{2,1,0:T(8,128)S(1)}, s32[2,8,64]{2,1,0:T(8,128)}, u32[]{:S(2)}) copy-start(s32[2,8,64]{2,1,0:T(8,128)} %param.16) | copy-start | bytes 12292
  3.9 31.1 %all-to-all-start = ((f32[2,2,4,64,512]{4,3,0,1,2:T(8,128)}), f32[2,2,4,64,512]{4,3,0,1,2:T(8,128)}, u32[]{:S(2)}, u32[]{:S(2)}) async-start(f32[2,2,4,64,512]{4,3,0,1,2:T(8,128)} %copy.115), calls=%async_computation | async-start | bytes 4194304 | tf_op jit(solution)/shard_map/all_to_all | solution.py:171
  9.4 30.4 %copy-start.24 = (f32[2,64,512]{2,1,0:T(8,128)}, f32[2,64,512]{2,1,0:T(8,128)S(1)}, u32[]{:S(2)}) copy-start(f32[2,64,512]{2,1,0:T(8,128)S(1)} %copy.114) | copy-start | bytes 786436
  40.0 9.4 %collective-permute-start = (f32[12,2,8,512]{3,2,1,0:T(8,128)S(1)}, f32[12,2,8,512]{3,2,1,0:T(8,128)S(1)}, u32[]{:S(2)}, u32[]{:S(2)}) collective-permute-start(f32[12,2,8,512]{3,2,1,0:T(8,128)S(1)} %get-tuple-element.93), channel_id=1, source_target_pairs={{0,32},{32,64},{64,96},{1,33},{33,65},{65,97},{2,34},{34,66},{66,9... | collective-permute-start | bytes 1179656 | tf_op jit(solution)/shard_map/ppermute | solution.py:52
  42.4 10.8 %collective-permute-start.1 = (f32[12,2,8,512]{3,2,1,0:T(8,128)S(1)}, f32[12,2,8,512]{3,2,1,0:T(8,128)S(1)}, u32[]{:S(2)}, u32[]{:S(2)}) collective-permute-start(f32[12,2,8,512]{3,2,1,0:T(8,128)S(1)} %get-tuple-element.94), channel_id=1, source_target_pairs={{32,0},{64,32},{96,64},{33,1},{65,33},{97,65},{34,2},{66,34},{98,6... | collective-permute-start | bytes 1179656 | tf_op jit(solution)/shard_map/ppermute | solution.py:53
  57.7 10.2 %collective-permute-start.2 = (f32[12,2,80,8]{2,3,1,0:T(8,128)}, f32[12,2,80,8]{2,3,1,0:T(8,128)}, u32[]{:S(2)}, u32[]{:S(2)}) collective-permute-start(f32[12,2,80,8]{2,3,1,0:T(8,128)} %copy.121), channel_id=1, source_target_pairs={{0,1},{1,2},{2,3},{3,4},{4,5},{5,6},{6,7},{7,8},{8,9},{9,10},{10,1... | collective-permute-start | bytes 184328 | tf_op jit(solution)/shard_map/ppermute | solution.py:52
  65.9 6.2 %collective-permute-start.3 = (f32[12,2,80,8]{2,3,1,0:T(8,128)}, f32[12,2,80,8]{2,3,1,0:T(8,128)}, u32[]{:S(2)}, u32[]{:S(2)}) collective-permute-start(f32[12,2,80,8]{2,3,1,0:T(8,128)} %copy.122), channel_id=1, source_target_pairs={{1,0},{2,1},{3,2},{4,3},{5,4},{6,5},{7,6},{8,7},{9,8},{10,9},{11,1... | collective-permute-start | bytes 184328 | tf_op jit(solution)/shard_map/ppermute | solution.py:53
  112.5 5.8 %copy-start.34 = (s32[32,64]{1,0:T(8,128)S(1)}, s32[32,64]{1,0:T(8,128)}, u32[]{:S(2)}) copy-start(s32[32,64]{1,0:T(8,128)} %param.14) | copy-start | bytes 24580
  112.5 16.7 %all-to-all-start.1 = ((f32[2,4,64,512]{3,2,0,1:T(8,128)}), f32[2,4,64,512]{3,2,0,1:T(8,128)S(1)}, u32[]{:S(2)}, u32[]{:S(2)}) async-start(f32[2,4,64,512]{3,2,0,1:T(8,128)} %pad_maximum_fusion.3), calls=%async_computation.1 | async-start | bytes 2097152 | tf_op jit(solution)/shard_map/all_to_all | solution.py:198
  116.3 14.0 %copy-start.20 = (f32[256,512]{0,1:T(8,128)}, f32[256,512]{0,1:T(8,128)S(1)}, u32[]{:S(2)}) copy-start(f32[256,512]{0,1:T(8,128)S(1)} %copy.157) | copy-start | bytes 1572868
  116.3 49.9 %collective-permute-start.10 = (f32[256,1]{0,1:T(1,128)S(1)}, f32[256,1]{0,1:T(1,128)S(1)}, u32[]{:S(2)}, u32[]{:S(2)}) collective-permute-start(f32[256,1]{0,1:T(1,128)S(1)} %get-tuple-element.169), channel_id=1, source_target_pairs={{1,0},{2,1},{3,2},{4,3},{5,4},{6,5},{7,6},{8,7},{9,8},{10,9},{11,1... | collective-permute-start | bytes 3080 | tf_op jit(solution)/shard_map/ppermute | solution.py:28
  135.5 15.1 %copy-start.32 = (f32[256,512]{1,0:T(8,128)S(1)}, f32[256,512]{1,0:T(8,128)}, u32[]{:S(2)}) copy-start(f32[256,512]{1,0:T(8,128)} %param.10) | copy-start | bytes 1572868
  137.0 18.4 %collective-permute-start.4 = (f32[3,1,512]{2,1,0:T(1,128)S(1)}, f32[3,1,512]{2,1,0:T(1,128)S(1)}, u32[]{:S(2)}, u32[]{:S(2)}) collective-permute-start(f32[3,1,512]{2,1,0:T(1,128)S(1)} %copy.139), channel_id=1, source_target_pairs={{0,32},{32,64},{64,96},{1,33},{33,65},{65,97},{2,34},{34,66},{66,9... | collective-permute-start | bytes 18440 | tf_op jit(solution)/shard_map/ppermute | solution.py:27
  140.5 17.3 %collective-permute-start.6 = (f32[3,1,512]{2,1,0:T(1,128)S(1)}, f32[3,1,512]{2,1,0:T(1,128)S(1)}, u32[]{:S(2)}, u32[]{:S(2)}) collective-permute-start(f32[3,1,512]{2,1,0:T(1,128)S(1)} %copy.141), channel_id=1, source_target_pairs={{32,0},{64,32},{96,64},{33,1},{65,33},{97,65},{34,2},{66,34},{98,6... | collective-permute-start | bytes 18440 | tf_op jit(solution)/shard_map/ppermute | solution.py:28
  141.9 9.8 %collective-permute-start.5 = (f32[3,256,1]{1,2,0:T(1,128)S(1)}, f32[3,256,1]{1,2,0:T(1,128)S(1)}, u32[]{:S(2)}, u32[]{:S(2)}) collective-permute-start(f32[3,256,1]{1,2,0:T(1,128)S(1)} %get-tuple-element.96), channel_id=1, source_target_pairs={{0,1},{1,2},{2,3},{3,4},{4,5},{5,6},{6,7},{7,8},{8,9},{9,10},{10,1... | collective-permute-start | bytes 9224 | tf_op jit(solution)/shard_map/ppermute | solution.py:27
  146.2 18.4 %collective-permute-start.7 = (f32[3,256,1]{1,2,0:T(1,128)S(1)}, f32[3,256,1]{1,2,0:T(1,128)S(1)}, u32[]{:S(2)}, u32[]{:S(2)}) collective-permute-start(f32[3,256,1]{1,2,0:T(1,128)S(1)} %get-tuple-element.95), channel_id=1, source_target_pairs={{1,0},{2,1},{3,2},{4,3},{5,4},{6,5},{7,6},{8,7},{9,8},{10,9},{11,1... | collective-permute-start | bytes 9224 | tf_op jit(solution)/shard_map/ppermute | solution.py:28
  151.6 14.6 %collective-permute-start.11 = (f32[256,1]{0,1:T(1,128)S(1)}, f32[256,1]{0,1:T(1,128)S(1)}, u32[]{:S(2)}, u32[]{:S(2)}) collective-permute-start(f32[256,1]{0,1:T(1,128)S(1)} %get-tuple-element.170), channel_id=1, source_target_pairs={{0,1},{1,2},{2,3},{3,4},{4,5},{5,6},{6,7},{7,8},{8,9},{9,10},{10,1... | collective-permute-start | bytes 3080 | tf_op jit(solution)/shard_map/ppermute | solution.py:27
  155.4 10.9 %collective-permute-start.8 = (f32[1,512]{0,1:T(8,128)}, f32[1,512]{0,1:T(8,128)S(1)}, u32[]{:S(2)}, u32[]{:S(2)}) collective-permute-start(f32[1,512]{0,1:T(8,128)} %copy.146), channel_id=1, source_target_pairs={{32,0},{64,32},{96,64},{33,1},{65,33},{97,65},{34,2},{66,34},{98,6... | collective-permute-start | bytes 6152 | tf_op jit(solution)/shard_map/ppermute | solution.py:28
  157.9 10.5 %collective-permute-start.9 = (f32[1,512]{0,1:T(8,128)}, f32[1,512]{0,1:T(8,128)}, u32[]{:S(2)}, u32[]{:S(2)}) collective-permute-start(f32[1,512]{0,1:T(8,128)} %copy.149), channel_id=1, source_target_pairs={{0,32},{32,64},{64,96},{1,33},{33,65},{65,97},{2,34},{34,66},{66,9... | collective-permute-start | bytes 6152 | tf_op jit(solution)/shard_map/ppermute | solution.py:27
  164.6 3.8 %copy-start.27 = (f32[256,512]{0,1:T(8,128)S(1)}, f32[256,512]{0,1:T(8,128)}, u32[]{:S(2)}) copy-start(f32[256,512]{0,1:T(8,128)} %copy.144) | copy-start | bytes 1572868
  171.8 13.8 %copy-start.4 = (f32[256,512]{0,1:T(8,128)}, f32[256,512]{0,1:T(8,128)S(1)}, u32[]{:S(2)}) copy-start(f32[256,512]{0,1:T(8,128)S(1)} %get-tuple-element.49) | copy-start | bytes 1572868
  171.8 13.8 %copy-start.6 = (f32[256,512]{0,1:T(8,128)}, f32[256,512]{0,1:T(8,128)S(1)}, u32[]{:S(2)}) copy-start(f32[256,512]{0,1:T(8,128)S(1)} %get-tuple-element.52) | copy-start | bytes 1572868
  171.8 13.8 %copy-start.9 = (f32[256,512]{0,1:T(8,128)}, f32[256,512]{0,1:T(8,128)S(1)}, u32[]{:S(2)}) copy-start(f32[256,512]{0,1:T(8,128)S(1)} %get-tuple-element.53) | copy-start | bytes 1572868
  171.8 13.8 %copy-start.12 = (f32[256,512]{0,1:T(8,128)}, f32[256,512]{0,1:T(8,128)S(1)}, u32[]{:S(2)}) copy-start(f32[256,512]{0,1:T(8,128)S(1)} %get-tuple-element.54) | copy-start | bytes 1572868
  171.8 13.8 %copy-start.15 = (f32[256,512]{0,1:T(8,128)}, f32[256,512]{0,1:T(8,128)S(1)}, u32[]{:S(2)}) copy-start(f32[256,512]{0,1:T(8,128)S(1)} %get-tuple-element.55) | copy-start | bytes 1572868
  171.9 12.4 %collective-permute-start.12 = (f32[1,512]{0,1:T(8,128)S(1)}, f32[1,512]{0,1:T(8,128)S(1)}, u32[]{:S(2)}, u32[]{:S(2)}) collective-permute-start(f32[1,512]{0,1:T(8,128)S(1)} %get-tuple-element.166), channel_id=1, source_target_pairs={{32,0},{64,32},{96,64},{33,1},{65,33},{97,65},{34,2},{66,34},{98,6... | collective-permute-start | bytes 6152 | tf_op jit(solution)/shard_map/ppermute | solution.py:28
  173.2 11.1 %collective-permute-start.13 = (f32[1,512]{0,1:T(8,128)S(1)}, f32[1,512]{0,1:T(8,128)S(1)}, u32[]{:S(2)}, u32[]{:S(2)}) collective-permute-start(f32[1,512]{0,1:T(8,128)S(1)} %get-tuple-element.165), channel_id=1, source_target_pairs={{0,32},{32,64},{64,96},{1,33},{33,65},{65,97},{2,34},{34,66},{66,9... | collective-permute-start | bytes 6152 | tf_op jit(solution)/shard_map/ppermute | solution.py:27
  177.7 5.9 %collective-permute-start.14 = (f32[256,1]{0,1:T(1,128)S(1)}, f32[256,1]{0,1:T(1,128)S(1)}, u32[]{:S(2)}, u32[]{:S(2)}) collective-permute-start(f32[256,1]{0,1:T(1,128)S(1)} %get-tuple-element.163), channel_id=1, source_target_pairs={{1,0},{2,1},{3,2},{4,3},{5,4},{6,5},{7,6},{8,7},{9,8},{10,9},{11,1... | collective-permute-start | bytes 3080 | tf_op jit(solution)/shard_map/ppermute | solution.py:28
  179.8 4.5 %collective-permute-start.15 = (f32[256,1]{0,1:T(1,128)S(1)}, f32[256,1]{0,1:T(1,128)S(1)}, u32[]{:S(2)}, u32[]{:S(2)}) collective-permute-start(f32[256,1]{0,1:T(1,128)S(1)} %get-tuple-element.164), channel_id=1, source_target_pairs={{0,1},{1,2},{2,3},{3,4},{4,5},{5,6},{6,7},{7,8},{8,9},{9,10},{10,1... | collective-permute-start | bytes 3080 | tf_op jit(solution)/shard_map/ppermute | solution.py:27
  226.5 13.9 %copy-start.7 = (f32[256,512]{0,1:T(8,128)S(1)}, f32[256,512]{0,1:T(8,128)}, u32[]{:S(2)}) copy-start(f32[256,512]{0,1:T(8,128)} %copy-done.6) | copy-start | bytes 1572868
  226.5 13.9 %copy-start.10 = (f32[256,512]{0,1:T(8,128)S(1)}, f32[256,512]{0,1:T(8,128)}, u32[]{:S(2)}) copy-start(f32[256,512]{0,1:T(8,128)} %copy-done.9) | copy-start | bytes 1572868
  226.5 13.9 %copy-start.13 = (f32[256,512]{0,1:T(8,128)S(1)}, f32[256,512]{0,1:T(8,128)}, u32[]{:S(2)}) copy-start(f32[256,512]{0,1:T(8,128)} %copy-done.12) | copy-start | bytes 1572868
  226.6 13.9 %copy-start.16 = (f32[256,512]{0,1:T(8,128)S(1)}, f32[256,512]{0,1:T(8,128)}, u32[]{:S(2)}) copy-start(f32[256,512]{0,1:T(8,128)} %copy-done.15) | copy-start | bytes 1572868
  228.0 12.4 %collective-permute-start.16 = (f32[1,512]{0,1:T(8,128)S(1)}, f32[1,512]{0,1:T(8,128)S(1)}, u32[]{:S(2)}, u32[]{:S(2)}) collective-permute-start(f32[1,512]{0,1:T(8,128)S(1)} %get-tuple-element.162), channel_id=1, source_target_pairs={{32,0},{64,32},{96,64},{33,1},{65,33},{97,65},{34,2},{66,34},{98,6... | collective-permute-start | bytes 6152 | tf_op jit(solution)/shard_map/ppermute | solution.py:28
  229.3 11.1 %collective-permute-start.17 = (f32[1,512]{0,1:T(8,128)S(1)}, f32[1,512]{0,1:T(8,128)S(1)}, u32[]{:S(2)}, u32[]{:S(2)}) collective-permute-start(f32[1,512]{0,1:T(8,128)S(1)} %get-tuple-element.161), channel_id=1, source_target_pairs={{0,32},{32,64},{64,96},{1,33},{33,65},{65,97},{2,34},{34,66},{66,9... | collective-permute-start | bytes 6152 | tf_op jit(solution)/shard_map/ppermute | solution.py:27
  233.3 6.4 %collective-permute-start.18 = (f32[256,1]{0,1:T(1,128)S(1)}, f32[256,1]{0,1:T(1,128)S(1)}, u32[]{:S(2)}, u32[]{:S(2)}) collective-permute-start(f32[256,1]{0,1:T(1,128)S(1)} %get-tuple-element.159), channel_id=1, source_target_pairs={{1,0},{2,1},{3,2},{4,3},{5,4},{6,5},{7,6},{8,7},{9,8},{10,9},{11,1... | collective-permute-start | bytes 3080 | tf_op jit(solution)/shard_map/ppermute | solution.py:28
  236.1 4.2 %collective-permute-start.19 = (f32[256,1]{0,1:T(1,128)S(1)}, f32[256,1]{0,1:T(1,128)S(1)}, u32[]{:S(2)}, u32[]{:S(2)}) collective-permute-start(f32[256,1]{0,1:T(1,128)S(1)} %get-tuple-element.160), channel_id=1, source_target_pairs={{0,1},{1,2},{2,3},{3,4},{4,5},{5,6},{6,7},{7,8},{8,9},{9,10},{10,1... | collective-permute-start | bytes 3080 | tf_op jit(solution)/shard_map/ppermute | solution.py:27
  283.0 13.2 %copy-start.26 = (f32[2,2,64,512]{3,2,0,1:T(8,128)S(1)}, f32[2,2,64,512]{3,2,0,1:T(8,128)}, u32[]{:S(2)}) copy-start(f32[2,2,64,512]{3,2,0,1:T(8,128)} %get-tuple-element.57) | copy-start | bytes 1572868
  283.1 13.9 %copy-start.8 = (f32[256,512]{0,1:T(8,128)S(1)}, f32[256,512]{0,1:T(8,128)}, u32[]{:S(2)}) copy-start(f32[256,512]{0,1:T(8,128)} %copy-done.6) | copy-start | bytes 1572868
  283.1 13.9 %copy-start.11 = (f32[256,512]{0,1:T(8,128)S(1)}, f32[256,512]{0,1:T(8,128)}, u32[]{:S(2)}) copy-start(f32[256,512]{0,1:T(8,128)} %copy-done.9) | copy-start | bytes 1572868
  283.1 13.9 %copy-start.14 = (f32[256,512]{0,1:T(8,128)S(1)}, f32[256,512]{0,1:T(8,128)}, u32[]{:S(2)}) copy-start(f32[256,512]{0,1:T(8,128)} %copy-done.12) | copy-start | bytes 1572868
  283.1 13.9 %copy-start.17 = (f32[256,512]{0,1:T(8,128)S(1)}, f32[256,512]{0,1:T(8,128)}, u32[]{:S(2)}) copy-start(f32[256,512]{0,1:T(8,128)} %copy-done.15) | copy-start | bytes 1572868
  283.1 13.8 %collective-permute-start.20 = (f32[1,512]{0,1:T(8,128)S(1)}, f32[1,512]{0,1:T(8,128)S(1)}, u32[]{:S(2)}, u32[]{:S(2)}) collective-permute-start(f32[1,512]{0,1:T(8,128)S(1)} %get-tuple-element.158), channel_id=1, source_target_pairs={{32,0},{64,32},{96,64},{33,1},{65,33},{97,65},{34,2},{66,34},{98,6... | collective-permute-start | bytes 6152 | tf_op jit(solution)/shard_map/ppermute | solution.py:28
  284.6 12.4 %collective-permute-start.21 = (f32[1,512]{0,1:T(8,128)S(1)}, f32[1,512]{0,1:T(8,128)S(1)}, u32[]{:S(2)}, u32[]{:S(2)}) collective-permute-start(f32[1,512]{0,1:T(8,128)S(1)} %get-tuple-element.157), channel_id=1, source_target_pairs={{0,32},{32,64},{64,96},{1,33},{33,65},{65,97},{2,34},{34,66},{66,9... | collective-permute-start | bytes 6152 | tf_op jit(solution)/shard_map/ppermute | solution.py:27
  288.6 8.3 %collective-permute-start.22 = (f32[256,1]{0,1:T(1,128)S(1)}, f32[256,1]{0,1:T(1,128)S(1)}, u32[]{:S(2)}, u32[]{:S(2)}) collective-permute-start(f32[256,1]{0,1:T(1,128)S(1)} %get-tuple-element.155), channel_id=1, source_target_pairs={{1,0},{2,1},{3,2},{4,3},{5,4},{6,5},{7,6},{8,7},{9,8},{10,9},{11,1... | collective-permute-start | bytes 3080 | tf_op jit(solution)/shard_map/ppermute | solution.py:28
  291.4 5.5 %collective-permute-start.23 = (f32[256,1]{0,1:T(1,128)S(1)}, f32[256,1]{0,1:T(1,128)S(1)}, u32[]{:S(2)}, u32[]{:S(2)}) collective-permute-start(f32[256,1]{0,1:T(1,128)S(1)} %get-tuple-element.156), channel_id=1, source_target_pairs={{0,1},{1,2},{2,3},{3,4},{4,5},{5,6},{6,7},{7,8},{8,9},{9,10},{10,1... | collective-permute-start | bytes 3080 | tf_op jit(solution)/shard_map/ppermute | solution.py:27
  297.0 38.1 %copy-start.5 = (f32[256,512]{0,1:T(8,128)S(1)}, f32[256,512]{0,1:T(8,128)}, u32[]{:S(2)}) copy-start(f32[256,512]{0,1:T(8,128)} %copy-done.4) | copy-start | bytes 1572868
  297.0 38.1 %copy-start.22 = (f32[256,512]{0,1:T(8,128)S(1)}, f32[256,512]{0,1:T(8,128)}, u32[]{:S(2)}) copy-start(f32[256,512]{0,1:T(8,128)} %copy-done.20) | copy-start | bytes 1572868
  (14 other events, 29.5 us)
where the time goes:
time: 342 us; the launch traced here: 337 us
  blocking collectives  107 us (31%)
  starting transfers between devices  77.7 us (23%)
  other arithmetic  56.2 us (16%)
  waiting for transfers between devices  44.4 us (13%)
  local copies, waits for them, and re-layouts  39.4 us (12%)
  between operations  11.7 us (3%)
    psum x12, blocking collectives, by_axis(): array = lax.psum(array, axis)  107 us
    ppermute x10, starting transfers between devices, with_halo(): lax.ppermute(last, axis, up)  39 us
    all_to_all x1, waiting for transfers between devices, shards(): lax.all_to_all(outgoing, 'grp', split_axis=2, concat_axis=2, tiled=True)  22.3 us
    ppermute x10, starting transfers between devices, with_halo(): lax.ppermute(first, axis, [(b, a) for a, b in up])  18.2 us
    unnamed x81, local copies, waits for them, and re-layouts  12.2 us
    ppermute x2, starting transfers between devices, extended(): before = lax.ppermute(last, axis, up)  8.51 us
    all_to_all x1, waiting for transfers between devices, shards(): lax.all_to_all(parcel, 'grp', split_axis=1, concat_axis=1, tiled=True)  7.65 us
  transfers between devices with their start and end apart: 26, of which 8 were waited for; matrix products, arithmetic and copies ran while one was open for 9% of the time, Pallas kernels for 0%

commit v1 on v0

--- a/solution.py
+++ b/solution.py
@@ -38,7 +38,8 @@
 
 def by_axis(array, axes):
     for axis in axes:
-        array = lax.psum(array, axis)
+        parts = lax.all_gather(array, axis)
+        array = jnp.sum(parts, axis=0)
     return array
 
 

time: 342 us -> 393 us (1.15)
  local copies, waits for them, and re-layouts: 39.4 us -> 77.4 us
  other arithmetic: 56.2 us -> 75 us
  blocking collectives: 107 us -> 100 us
    psum x12 -> x0, blocking collectives: 107 us -> none  [by_axis(): array = lax.psum(array, axis)]
    unnamed x0 -> x12, blocking collectives: none -> 100 us
    unnamed x81 -> x131, local copies, waits for them, and re-layouts: 12.2 us -> 49.4 us
    reduce_sum x0 -> x24, other arithmetic: none -> 15.3 us  [by_axis(): array = jnp.sum(parts, axis=0)]
  transfers between devices with their start and end apart: 26 -> 26, of which waited for: 8 -> 9; matrix products, arithmetic and copies ran while one was open for 9% -> 7% of each run, Pallas kernels for 0% -> 0%
where the time goes in v1:
time: 393 us; the launch traced here: 387 us
  blocking collectives  100 us (25%)
  starting transfers between devices  77.8 us (20%)
  local copies, waits for them, and re-layouts  77.4 us (20%)
  other arithmetic  75 us (19%)
  waiting for transfers between devices  44.4 us (11%)
  between operations  11.7 us (3%)
    unnamed x12, blocking collectives  100 us
    unnamed x131, local copies, waits for them, and re-layouts  49.4 us
    ppermute x10, starting transfers between devices, with_halo(): lax.ppermute(last, axis, up)  39.3 us
    all_to_all x1, waiting for transfers between devices, shards(): lax.all_to_all(outgoing, 'grp', split_axis=2, concat_axis=2, tiled=True)  22.3 us
    ppermute x10, starting transfers between devices, with_halo(): lax.ppermute(first, axis, [(b, a) for a, b in up])  18 us
    reduce_sum x24, other arithmetic, by_axis(): array = jnp.sum(parts, axis=0)  15.3 us
    ppermute x2, starting transfers between devices, extended(): before = lax.ppermute(last, axis, up)  8.52 us
  transfers between devices with their start and end apart: 26, of which 9 were waited for; matrix products, arithmetic and copies ran while one was open for 7% of the time, Pallas kernels for 0%

profile of v1, /device:TPU:1, one launch (start us, length us, event | category | flops | bytes accessed | tf_op | source)
XLA Modules:
  0.0 386.6 jit_solution(14146664448258719174)
XLA Ops:
  3.9 5.1 %all-to-all-start = ((f32[2,2,4,64,512]{4,3,0,1,2:T(8,128)}), f32[2,2,4,64,512]{4,3,0,1,2:T(8,128)}, u32[]{:S(2)}, u32[]{:S(2)}) async-start(f32[2,2,4,64,512]{4,3,0,1,2:T(8,128)} %copy.115), calls=%async_computation | async-start | bytes 4194304 | tf_op jit(solution)/shard_map/all_to_all | solution.py:172
  12.7 22.3 %all-to-all-done = f32[2,2,4,64,512]{4,3,0,1,2:T(8,128)} async-done(((f32[2,2,4,64,512]{4,3,0,1,2:T(8,128)}), f32[2,2,4,64,512]{4,3,0,1,2:T(8,128)}, u32[]{:S(2)}, u32[]{:S(2)}) %all-to-all-start) | async-done | bytes 2097184 | tf_op jit(solution)/shard_map/all_to_all | solution.py:172
  35.0 2.7 reduce_sum.279
  39.9 2.4 collective-permute-start
  43.7 5.6 %collective-permute-done = f32[12,2,8,512]{3,2,1,0:T(8,128)S(1)} collective-permute-done((f32[12,2,8,512]{3,2,1,0:T(8,128)S(1)}, f32[12,2,8,512]{3,2,1,0:T(8,128)S(1)}, u32[]{:S(2)}, u32[]{:S(2)}) %collective-permute-start) | collective-permute-done | bytes 393248 | tf_op jit(solution)/shard_map/ppermute | solution.py:53
  49.3 3.9 collective-permute-done.1
  55.6 2.1 copy.121
  57.7 6.1 %collective-permute-start.2 = (f32[12,2,80,8]{2,3,1,0:T(8,128)}, f32[12,2,80,8]{2,3,1,0:T(8,128)}, u32[]{:S(2)}, u32[]{:S(2)}) collective-permute-start(f32[12,2,80,8]{2,3,1,0:T(8,128)} %copy.121), channel_id=1, source_target_pairs={{0,1},{1,2},{2,3},{3,4},{4,5},{5,6},{6,7},{7,8},{8,9},{9,10},{10,1... | collective-permute-start | bytes 184328 | tf_op jit(solution)/shard_map/ppermute | solution.py:53
  63.8 2.1 copy.122
  65.9 1.9 collective-permute-start.3
  67.9 2.2 copy.123
  70.1 2.0 collective-permute-done.3
  72.2 2.2 copy.124
  74.4 4.6 %pad_maximum_fusion = f32[12,2,80,528]{3,2,1,0:T(8,128)S(1)} fusion(f32[12,2,80,8]{3,2,1,0:T(8,128)} %copy.124, f32[12,2,8,512]{3,2,1,0:T(8,128)} %copy-done.2, f32[12,2,64,512]{3,2,1,0:T(8,128)S(1)} %constant_dynamic-update-slice_fusion, f32[12,2,8,512]{3,2,1,0:T(8,128)S(1)} %collective-permute-done, f32[12,2,80,8]{3,2,1,0:T(8,128)} %copy.123), kind=kLoop, calls=%fused_computation | loop fusion | flops 4055040 | bytes 8110080 | tf_op jit(solution)/shard_map/concatenate | solution.py:55
  112.6 3.6 all-to-all-start.1
  116.5 1.9 collective-permute-start.10
  118.5 2.0 copy.138
  121.7 7.6 %all-to-all-done.1 = f32[2,4,64,512]{3,2,0,1:T(8,128)S(1)} async-done(((f32[2,4,64,512]{3,2,0,1:T(8,128)}), f32[2,4,64,512]{3,2,0,1:T(8,128)S(1)}, u32[]{:S(2)}, u32[]{:S(2)}) %all-to-all-start.1) | async-done | bytes 1048608 | tf_op jit(solution)/shard_map/all_to_all | solution.py:199
  130.4 2.5 copy.137
  137.1 2.2 collective-permute-start.4
  142.0 4.4 %collective-permute-start.5 = (f32[3,256,1]{1,2,0:T(1,128)S(1)}, f32[3,256,1]{1,2,0:T(1,128)S(1)}, u32[]{:S(2)}, u32[]{:S(2)}) collective-permute-start(f32[3,256,1]{1,2,0:T(1,128)S(1)} %get-tuple-element.96), channel_id=1, source_target_pairs={{0,1},{1,2},{2,3},{3,4},{4,5},{5,6},{6,7},{7,8},{8,9},{9,10},{10,1... | collective-permute-start | bytes 9224 | tf_op jit(solution)/shard_map/ppermute | solution.py:27
  146.3 1.9 collective-permute-start.7
  151.7 3.6 collective-permute-start.11
  157.9 5.6 %collective-permute-start.9 = (f32[1,512]{0,1:T(8,128)}, f32[1,512]{0,1:T(8,128)}, u32[]{:S(2)}, u32[]{:S(2)}) collective-permute-start(f32[1,512]{0,1:T(8,128)} %copy.149), channel_id=1, source_target_pairs={{0,32},{32,64},{64,96},{1,33},{33,65},{65,97},{2,34},{34,66},{66,9... | collective-permute-start | bytes 6152 | tf_op jit(solution)/shard_map/ppermute | solution.py:27
  168.5 4.1 %fusion.196 = (f32[256,512]{0,1:T(8,128)S(1)}, f32[256,512]{0,1:T(8,128)S(1)}, f32[256,512]{0,1:T(8,128)}, f32[256,512]{0,1:T(8,128)}, f32[256,512]{0,1:T(8,128)}, /*index=5*/f32[256,512]{0,1:T(8,128)}, f32[256,512]{0,1:T(8,128)}) fusion(f32[256,512]{0,1:T(8,128)S(1)} %copy-done.18, f32[1,512]{0,1:T(8,128)} %copy-done.29, ...), kind=kLoop, calls=%fused_computation.471 | loop fusion | flops 6291456 | bytes 11610624 | tf_op jit(solution)/shard_map/div | solution.py:218
  174.7 4.5 %collective-permute-start.13 = (f32[1,512]{0,1:T(8,128)}, f32[1,512]{0,1:T(8,128)S(1)}, u32[]{:S(2)}, u32[]{:S(2)}) collective-permute-start(f32[1,512]{0,1:T(8,128)} %get-tuple-element.165), channel_id=1, source_target_pairs={{0,32},{32,64},{64,96},{1,33},{33,65},{65,97},{2,34},{34,66},{66,9... | collective-permute-start | bytes 6152 | tf_op jit(solution)/shard_map/ppermute | solution.py:27
  179.2 2.1 collective-permute-start.14
  181.3 3.7 collective-permute-start.15
  186.6 3.9 %multiply_reduce_fusion.3 = (f32[]{:T(128)}, f32[]{:T(128)}, f32[256,512]{0,1:T(8,128)S(1)}) fusion(f32[256,512]{0,1:T(8,128)} %copy-done.4, f32[256,512]{0,1:T(8,128)S(1)} %get-tuple-element.50, f32[256,512]{0,1:T(8,128)} %get-tuple-element.55, f32[1,512]{0,1:T(8,128)} %copy-done.30, f32[1,512]{0,1:T(8,128)} %copy-done.31, ...), kind=kLoop, calls=%fused_computation.229 | loop fusion | flops 4063230 | bytes 3676168 | tf_op jit(solution)/shard_map/reduce_sum | solution.py:134
  193.8 9.2 %all-reduce.58 = (f32[4]{0:T(128)S(1)}, f32[4]{0:T(128)S(1)}) all-reduce(f32[4]{0:T(128)S(1)} %dynamic-update-slice, f32[4]{0:T(128)S(1)} %dynamic-update-slice.4), channel_id=1, replica_groups=mesh['grp'=4,'tile_0'=4,'tile_1'=4,'tile_2'=2] {'grp'}, use_global_device_ids=true, to_apply=%add.26 | all-reduce | flops 8 | bytes 64
  207.6 9.5 %all-reduce.55 = (f32[4]{0:T(128)S(1)}, f32[4]{0:T(128)S(1)}) all-reduce(f32[4]{0:T(128)S(1)} %dynamic-update-slice.1, f32[4]{0:T(128)S(1)} %dynamic-update-slice.5), channel_id=1, replica_groups=mesh['grp'=4,'tile_0'=4,'tile_1'=4,'tile_2'=2] {'tile_0'}, use_global_device_ids=true, to_apply=%add.27 | all-reduce | flops 8 | bytes 64
  221.6 8.6 %all-reduce.52 = (f32[4]{0:T(128)S(1)}, f32[4]{0:T(128)S(1)}) all-reduce(f32[4]{0:T(128)S(1)} %dynamic-update-slice.2, f32[4]{0:T(128)S(1)} %dynamic-update-slice.6), channel_id=1, replica_groups=mesh['grp'=4,'tile_0'=4,'tile_1'=4,'tile_2'=2] {'tile_1'}, use_global_device_ids=true, to_apply=%add.28 | all-reduce | flops 8 | bytes 64
  234.3 9.7 %all-reduce.61 = (f32[2]{0:T(128)S(1)}, f32[2]{0:T(128)S(1)}) all-reduce(f32[2]{0:T(128)S(1)} %dynamic-update-slice.3, f32[2]{0:T(128)S(1)} %dynamic-update-slice.7), channel_id=1, replica_groups=mesh['grp'=4,'tile_0'=4,'tile_1'=4,'tile_2'=2] {'tile_2'}, use_global_device_ids=true, to_apply=%add.29 | all-reduce | flops 4 | bytes 32
  249.4 4.3 %collective-permute-start.17 = (f32[1,512]{0,1:T(8,128)S(1)}, f32[1,512]{0,1:T(8,128)S(1)}, u32[]{:S(2)}, u32[]{:S(2)}) collective-permute-start(f32[1,512]{0,1:T(8,128)S(1)} %get-tuple-element.161), channel_id=1, source_target_pairs={{0,32},{32,64},{64,96},{1,33},{33,65},{65,97},{2,34},{34,66},{66,9... | collective-permute-start | bytes 6152 | tf_op jit(solution)/shard_map/ppermute | solution.py:27
  253.6 2.8 collective-permute-start.18
  256.4 3.5 collective-permute-start.19
  260.7 2.1 multiply_reduce_fusion.1
  265.6 6.8 %all-reduce.57 = (f32[4]{0:T(128)S(1)}, f32[4]{0:T(128)S(1)}) all-reduce(f32[4]{0:T(128)S(1)} %dynamic-update-slice.8, f32[4]{0:T(128)S(1)} %dynamic-update-slice.12), channel_id=1, replica_groups=mesh['grp'=4,'tile_0'=4,'tile_1'=4,'tile_2'=2] {'grp'}, use_global_device_ids=true, to_apply=%add.34 | all-reduce | flops 8 | bytes 64
  276.5 6.7 %all-reduce.54 = (f32[4]{0:T(128)S(1)}, f32[4]{0:T(128)S(1)}) all-reduce(f32[4]{0:T(128)S(1)} %dynamic-update-slice.9, f32[4]{0:T(128)S(1)} %dynamic-update-slice.13), channel_id=1, replica_groups=mesh['grp'=4,'tile_0'=4,'tile_1'=4,'tile_2'=2] {'tile_0'}, use_global_device_ids=true, to_apply=%add.35 | all-reduce | flops 8 | bytes 64
  287.1 8.4 %all-reduce.51 = (f32[4]{0:T(128)S(1)}, f32[4]{0:T(128)S(1)}) all-reduce(f32[4]{0:T(128)S(1)} %dynamic-update-slice.10, f32[4]{0:T(128)S(1)} %dynamic-update-slice.14), channel_id=1, replica_groups=mesh['grp'=4,'tile_0'=4,'tile_1'=4,'tile_2'=2] {'tile_1'}, use_global_device_ids=true, to_apply=%add.36 | all-reduce | flops 8 | bytes 64
  299.7 9.9 %all-reduce.60 = (f32[2]{0:T(128)S(1)}, f32[2]{0:T(128)S(1)}) all-reduce(f32[2]{0:T(128)S(1)} %dynamic-update-slice.11, f32[2]{0:T(128)S(1)} %dynamic-update-slice.15), channel_id=1, replica_groups=mesh['grp'=4,'tile_0'=4,'tile_1'=4,'tile_2'=2] {'tile_2'}, use_global_device_ids=true, to_apply=%add.37 | all-reduce | flops 4 | bytes 32
  318.2 4.0 %collective-permute-start.21 = (f32[1,512]{0,1:T(8,128)S(1)}, f32[1,512]{0,1:T(8,128)S(1)}, u32[]{:S(2)}, u32[]{:S(2)}) collective-permute-start(f32[1,512]{0,1:T(8,128)S(1)} %get-tuple-element.157), channel_id=1, source_target_pairs={{0,32},{32,64},{64,96},{1,33},{33,65},{65,97},{2,34},{34,66},{66,9... | collective-permute-start | bytes 6152 | tf_op jit(solution)/shard_map/ppermute | solution.py:27
  322.2 2.8 collective-permute-start.22
  325.1 3.5 collective-permute-start.23
  333.4 6.6 %all-reduce.56 = (f32[4]{0:T(128)S(1)}, f32[4]{0:T(128)S(1)}) all-reduce(f32[4]{0:T(128)S(1)} %dynamic-update-slice.16, f32[4]{0:T(128)S(1)} %dynamic-update-slice.20), channel_id=1, replica_groups=mesh['grp'=4,'tile_0'=4,'tile_1'=4,'tile_2'=2] {'grp'}, use_global_device_ids=true, to_apply=%add.42 | all-reduce | flops 8 | bytes 64
  344.0 6.7 %all-reduce.53 = (f32[4]{0:T(128)S(1)}, f32[4]{0:T(128)S(1)}) all-reduce(f32[4]{0:T(128)S(1)} %dynamic-update-slice.17, f32[4]{0:T(128)S(1)} %dynamic-update-slice.21), channel_id=1, replica_groups=mesh['grp'=4,'tile_0'=4,'tile_1'=4,'tile_2'=2] {'tile_0'}, use_global_device_ids=true, to_apply=%add.43 | all-reduce | flops 8 | bytes 64
  355.7 8.3 %all-reduce.50 = (f32[4]{0:T(128)S(1)}, f32[4]{0:T(128)S(1)}) all-reduce(f32[4]{0:T(128)S(1)} %dynamic-update-slice.18, f32[4]{0:T(128)S(1)} %dynamic-update-slice.22), channel_id=1, replica_groups=mesh['grp'=4,'tile_0'=4,'tile_1'=4,'tile_2'=2] {'tile_1'}, use_global_device_ids=true, to_apply=%add.44 | all-reduce | flops 8 | bytes 64
  369.9 10.0 %all-reduce.59 = (f32[2]{0:T(128)S(1)}, f32[2]{0:T(128)S(1)}) all-reduce(f32[2]{0:T(128)S(1)} %dynamic-update-slice.19, f32[2]{0:T(128)S(1)} %dynamic-update-slice.23), channel_id=1, replica_groups=mesh['grp'=4,'tile_0'=4,'tile_1'=4,'tile_2'=2] {'tile_2'}, use_global_device_ids=true, to_apply=%add.45 | all-reduce | flops 4 | bytes 32
  (310 shorter events, 132.5 us)
Async XLA Ops:
  3.9 5.1 %copy-start.33 = (s32[2,8,64]{2,1,0:T(8,128)S(1)}, s32[2,8,64]{2,1,0:T(8,128)}, u32[]{:S(2)}) copy-start(s32[2,8,64]{2,1,0:T(8,128)} %param.16) | copy-start | bytes 12292
  3.9 31.1 %all-to-all-start = ((f32[2,2,4,64,512]{4,3,0,1,2:T(8,128)}), f32[2,2,4,64,512]{4,3,0,1,2:T(8,128)}, u32[]{:S(2)}, u32[]{:S(2)}) async-start(f32[2,2,4,64,512]{4,3,0,1,2:T(8,128)} %copy.115), calls=%async_computation | async-start | bytes 4194304 | tf_op jit(solution)/shard_map/all_to_all | solution.py:172
  9.4 30.4 %copy-start.21 = (f32[2,64,512]{2,1,0:T(8,128)}, f32[2,64,512]{2,1,0:T(8,128)S(1)}, u32[]{:S(2)}) copy-start(f32[2,64,512]{2,1,0:T(8,128)S(1)} %copy.114) | copy-start | bytes 786436
  39.9 9.4 %collective-permute-start = (f32[12,2,8,512]{3,2,1,0:T(8,128)S(1)}, f32[12,2,8,512]{3,2,1,0:T(8,128)S(1)}, u32[]{:S(2)}, u32[]{:S(2)}) collective-permute-start(f32[12,2,8,512]{3,2,1,0:T(8,128)S(1)} %get-tuple-element.93), channel_id=1, source_target_pairs={{0,32},{32,64},{64,96},{1,33},{33,65},{65,97},{2,34},{34,66},{66,9... | collective-permute-start | bytes 1179656 | tf_op jit(solution)/shard_map/ppermute | solution.py:53
  42.4 10.8 %collective-permute-start.1 = (f32[12,2,8,512]{3,2,1,0:T(8,128)S(1)}, f32[12,2,8,512]{3,2,1,0:T(8,128)S(1)}, u32[]{:S(2)}, u32[]{:S(2)}) collective-permute-start(f32[12,2,8,512]{3,2,1,0:T(8,128)S(1)} %get-tuple-element.94), channel_id=1, source_target_pairs={{32,0},{64,32},{96,64},{33,1},{65,33},{97,65},{34,2},{66,34},{98,6... | collective-permute-start | bytes 1179656 | tf_op jit(solution)/shard_map/ppermute | solution.py:54
  57.7 10.2 %collective-permute-start.2 = (f32[12,2,80,8]{2,3,1,0:T(8,128)}, f32[12,2,80,8]{2,3,1,0:T(8,128)}, u32[]{:S(2)}, u32[]{:S(2)}) collective-permute-start(f32[12,2,80,8]{2,3,1,0:T(8,128)} %copy.121), channel_id=1, source_target_pairs={{0,1},{1,2},{2,3},{3,4},{4,5},{5,6},{6,7},{7,8},{8,9},{9,10},{10,1... | collective-permute-start | bytes 184328 | tf_op jit(solution)/shard_map/ppermute | solution.py:53
  65.9 6.2 %collective-permute-start.3 = (f32[12,2,80,8]{2,3,1,0:T(8,128)}, f32[12,2,80,8]{2,3,1,0:T(8,128)}, u32[]{:S(2)}, u32[]{:S(2)}) collective-permute-start(f32[12,2,80,8]{2,3,1,0:T(8,128)} %copy.122), channel_id=1, source_target_pairs={{1,0},{2,1},{3,2},{4,3},{5,4},{6,5},{7,6},{8,7},{9,8},{10,9},{11,1... | collective-permute-start | bytes 184328 | tf_op jit(solution)/shard_map/ppermute | solution.py:54
  112.6 5.8 %copy-start.32 = (s32[32,64]{1,0:T(8,128)S(1)}, s32[32,64]{1,0:T(8,128)}, u32[]{:S(2)}) copy-start(s32[32,64]{1,0:T(8,128)} %param.14) | copy-start | bytes 24580
  112.6 16.7 %all-to-all-start.1 = ((f32[2,4,64,512]{3,2,0,1:T(8,128)}), f32[2,4,64,512]{3,2,0,1:T(8,128)S(1)}, u32[]{:S(2)}, u32[]{:S(2)}) async-start(f32[2,4,64,512]{3,2,0,1:T(8,128)} %pad_maximum_fusion.3), calls=%async_computation.1 | async-start | bytes 2097152 | tf_op jit(solution)/shard_map/all_to_all | solution.py:199
  116.4 14.0 %copy-start.17 = (f32[256,512]{0,1:T(8,128)}, f32[256,512]{0,1:T(8,128)S(1)}, u32[]{:S(2)}) copy-start(f32[256,512]{0,1:T(8,128)S(1)} %copy.157) | copy-start | bytes 1572868
  116.5 49.8 %collective-permute-start.10 = (f32[256,1]{0,1:T(1,128)S(1)}, f32[256,1]{0,1:T(1,128)S(1)}, u32[]{:S(2)}, u32[]{:S(2)}) collective-permute-start(f32[256,1]{0,1:T(1,128)S(1)} %get-tuple-element.169), channel_id=1, source_target_pairs={{1,0},{2,1},{3,2},{4,3},{5,4},{6,5},{7,6},{8,7},{9,8},{10,9},{11,1... | collective-permute-start | bytes 3080 | tf_op jit(solution)/shard_map/ppermute | solution.py:28
  135.6 15.1 %copy-start.28 = (f32[256,512]{1,0:T(8,128)S(1)}, f32[256,512]{1,0:T(8,128)}, u32[]{:S(2)}) copy-start(f32[256,512]{1,0:T(8,128)} %param.10) | copy-start | bytes 1572868
  137.1 18.4 %collective-permute-start.4 = (f32[3,1,512]{2,1,0:T(1,128)S(1)}, f32[3,1,512]{2,1,0:T(1,128)S(1)}, u32[]{:S(2)}, u32[]{:S(2)}) collective-permute-start(f32[3,1,512]{2,1,0:T(1,128)S(1)} %copy.139), channel_id=1, source_target_pairs={{0,32},{32,64},{64,96},{1,33},{33,65},{65,97},{2,34},{34,66},{66,9... | collective-permute-start | bytes 18440 | tf_op jit(solution)/shard_map/ppermute | solution.py:27
  140.7 17.3 %collective-permute-start.6 = (f32[3,1,512]{2,1,0:T(1,128)S(1)}, f32[3,1,512]{2,1,0:T(1,128)S(1)}, u32[]{:S(2)}, u32[]{:S(2)}) collective-permute-start(f32[3,1,512]{2,1,0:T(1,128)S(1)} %copy.141), channel_id=1, source_target_pairs={{32,0},{64,32},{96,64},{33,1},{65,33},{97,65},{34,2},{66,34},{98,6... | collective-permute-start | bytes 18440 | tf_op jit(solution)/shard_map/ppermute | solution.py:28
  142.0 9.7 %collective-permute-start.5 = (f32[3,256,1]{1,2,0:T(1,128)S(1)}, f32[3,256,1]{1,2,0:T(1,128)S(1)}, u32[]{:S(2)}, u32[]{:S(2)}) collective-permute-start(f32[3,256,1]{1,2,0:T(1,128)S(1)} %get-tuple-element.96), channel_id=1, source_target_pairs={{0,1},{1,2},{2,3},{3,4},{4,5},{5,6},{6,7},{7,8},{8,9},{9,10},{10,1... | collective-permute-start | bytes 9224 | tf_op jit(solution)/shard_map/ppermute | solution.py:27
  146.3 18.4 %collective-permute-start.7 = (f32[3,256,1]{1,2,0:T(1,128)S(1)}, f32[3,256,1]{1,2,0:T(1,128)S(1)}, u32[]{:S(2)}, u32[]{:S(2)}) collective-permute-start(f32[3,256,1]{1,2,0:T(1,128)S(1)} %get-tuple-element.95), channel_id=1, source_target_pairs={{1,0},{2,1},{3,2},{4,3},{5,4},{6,5},{7,6},{8,7},{9,8},{10,9},{11,1... | collective-permute-start | bytes 9224 | tf_op jit(solution)/shard_map/ppermute | solution.py:28
  151.7 14.6 %collective-permute-start.11 = (f32[256,1]{0,1:T(1,128)S(1)}, f32[256,1]{0,1:T(1,128)S(1)}, u32[]{:S(2)}, u32[]{:S(2)}) collective-permute-start(f32[256,1]{0,1:T(1,128)S(1)} %get-tuple-element.170), channel_id=1, source_target_pairs={{0,1},{1,2},{2,3},{3,4},{4,5},{5,6},{6,7},{7,8},{8,9},{9,10},{10,1... | collective-permute-start | bytes 3080 | tf_op jit(solution)/shard_map/ppermute | solution.py:27
  155.4 10.9 %collective-permute-start.8 = (f32[1,512]{0,1:T(8,128)}, f32[1,512]{0,1:T(8,128)S(1)}, u32[]{:S(2)}, u32[]{:S(2)}) collective-permute-start(f32[1,512]{0,1:T(8,128)} %copy.146), channel_id=1, source_target_pairs={{32,0},{64,32},{96,64},{33,1},{65,33},{97,65},{34,2},{66,34},{98,6... | collective-permute-start | bytes 6152 | tf_op jit(solution)/shard_map/ppermute | solution.py:28
  157.9 10.5 %collective-permute-start.9 = (f32[1,512]{0,1:T(8,128)}, f32[1,512]{0,1:T(8,128)}, u32[]{:S(2)}, u32[]{:S(2)}) collective-permute-start(f32[1,512]{0,1:T(8,128)} %copy.149), channel_id=1, source_target_pairs={{0,32},{32,64},{64,96},{1,33},{33,65},{65,97},{2,34},{34,66},{66,9... | collective-permute-start | bytes 6152 | tf_op jit(solution)/shard_map/ppermute | solution.py:27
  164.7 3.8 copy-start.23
  166.3 18.8 %copy-start.37 = (u32[128]{0:T(128)S(1)}, u32[128]{0:T(128)}, u32[]{:S(2)}) copy-start(u32[128]{0:T(128)} %constant.90) | copy-start | bytes 1540
  172.5 6.6 %copy-start.4 = (f32[256,512]{0,1:T(8,128)}, f32[256,512]{0,1:T(8,128)S(1)}, u32[]{:S(2)}) copy-start(f32[256,512]{0,1:T(8,128)S(1)} %get-tuple-element.49) | copy-start | bytes 1572868
  172.6 14.0 %copy-start.6 = (f32[256,512]{0,1:T(8,128)S(1)}, f32[256,512]{0,1:T(8,128)}, u32[]{:S(2)}) copy-start(f32[256,512]{0,1:T(8,128)} %get-tuple-element.52) | copy-start | bytes 1572868
  172.6 14.0 %copy-start.8 = (f32[256,512]{0,1:T(8,128)S(1)}, f32[256,512]{0,1:T(8,128)}, u32[]{:S(2)}) copy-start(f32[256,512]{0,1:T(8,128)} %get-tuple-element.53) | copy-start | bytes 1572868
  173.4 12.4 %collective-permute-start.12 = (f32[1,512]{0,1:T(8,128)}, f32[1,512]{0,1:T(8,128)S(1)}, u32[]{:S(2)}, u32[]{:S(2)}) collective-permute-start(f32[1,512]{0,1:T(8,128)} %get-tuple-element.166), channel_id=1, source_target_pairs={{32,0},{64,32},{96,64},{33,1},{65,33},{97,65},{34,2},{66,34},{98,6... | collective-permute-start | bytes 6152 | tf_op jit(solution)/shard_map/ppermute | solution.py:28
  174.7 11.1 %collective-permute-start.13 = (f32[1,512]{0,1:T(8,128)}, f32[1,512]{0,1:T(8,128)S(1)}, u32[]{:S(2)}, u32[]{:S(2)}) collective-permute-start(f32[1,512]{0,1:T(8,128)} %get-tuple-element.165), channel_id=1, source_target_pairs={{0,32},{32,64},{64,96},{1,33},{33,65},{65,97},{2,34},{34,66},{66,9... | collective-permute-start | bytes 6152 | tf_op jit(solution)/shard_map/ppermute | solution.py:27
  179.2 6.5 %collective-permute-start.14 = (f32[256,1]{0,1:T(1,128)S(1)}, f32[256,1]{0,1:T(1,128)S(1)}, u32[]{:S(2)}, u32[]{:S(2)}) collective-permute-start(f32[256,1]{0,1:T(1,128)S(1)} %get-tuple-element.163), channel_id=1, source_target_pairs={{1,0},{2,1},{3,2},{4,3},{5,4},{6,5},{7,6},{8,7},{9,8},{10,9},{11,1... | collective-permute-start | bytes 3080 | tf_op jit(solution)/shard_map/ppermute | solution.py:28
  181.3 4.5 %collective-permute-start.15 = (f32[256,1]{0,1:T(1,128)S(1)}, f32[256,1]{0,1:T(1,128)S(1)}, u32[]{:S(2)}, u32[]{:S(2)}) collective-permute-start(f32[256,1]{0,1:T(1,128)S(1)} %get-tuple-element.164), channel_id=1, source_target_pairs={{0,1},{1,2},{2,3},{3,4},{4,5},{5,6},{6,7},{7,8},{8,9},{9,10},{10,1... | collective-permute-start | bytes 3080 | tf_op jit(solution)/shard_map/ppermute | solution.py:27
  186.6 6.6 %copy-start.36 = (u32[128]{0:T(128)S(1)}, u32[128]{0:T(128)}, u32[]{:S(2)}) copy-start(u32[128]{0:T(128)} %constant.95) | copy-start | bytes 1540
  186.6 20.4 %copy-start.35 = (u32[128]{0:T(128)S(1)}, u32[128]{0:T(128)}, u32[]{:S(2)}) copy-start(u32[128]{0:T(128)} %constant.100) | copy-start | bytes 1540
  186.6 34.4 %copy-start.34 = (u32[128]{0:T(128)S(1)}, u32[128]{0:T(128)}, u32[]{:S(2)}) copy-start(u32[128]{0:T(128)} %constant.105) | copy-start | bytes 1540
  246.6 14.1 %copy-start.9 = (f32[256,512]{0,1:T(8,128)S(1)}, f32[256,512]{0,1:T(8,128)}, u32[]{:S(2)}) copy-start(f32[256,512]{0,1:T(8,128)} %get-tuple-element.53) | copy-start | bytes 1572868
  246.6 14.1 %copy-start.11 = (f32[256,512]{0,1:T(8,128)S(1)}, f32[256,512]{0,1:T(8,128)}, u32[]{:S(2)}) copy-start(f32[256,512]{0,1:T(8,128)} %get-tuple-element.54) | copy-start | bytes 1572868
  246.6 14.1 %copy-start.13 = (f32[256,512]{0,1:T(8,128)S(1)}, f32[256,512]{0,1:T(8,128)}, u32[]{:S(2)}) copy-start(f32[256,512]{0,1:T(8,128)} %get-tuple-element.55) | copy-start | bytes 1572868
  248.1 12.6 %collective-permute-start.16 = (f32[1,512]{0,1:T(8,128)S(1)}, f32[1,512]{0,1:T(8,128)S(1)}, u32[]{:S(2)}, u32[]{:S(2)}) collective-permute-start(f32[1,512]{0,1:T(8,128)S(1)} %get-tuple-element.162), channel_id=1, source_target_pairs={{32,0},{64,32},{96,64},{33,1},{65,33},{97,65},{34,2},{66,34},{98,6... | collective-permute-start | bytes 6152 | tf_op jit(solution)/shard_map/ppermute | solution.py:28
  249.4 11.3 %collective-permute-start.17 = (f32[1,512]{0,1:T(8,128)S(1)}, f32[1,512]{0,1:T(8,128)S(1)}, u32[]{:S(2)}, u32[]{:S(2)}) collective-permute-start(f32[1,512]{0,1:T(8,128)S(1)} %get-tuple-element.161), channel_id=1, source_target_pairs={{0,32},{32,64},{64,96},{1,33},{33,65},{65,97},{2,34},{34,66},{66,9... | collective-permute-start | bytes 6152 | tf_op jit(solution)/shard_map/ppermute | solution.py:27
  253.6 6.4 %collective-permute-start.18 = (f32[256,1]{0,1:T(1,128)S(1)}, f32[256,1]{0,1:T(1,128)S(1)}, u32[]{:S(2)}, u32[]{:S(2)}) collective-permute-start(f32[256,1]{0,1:T(1,128)S(1)} %get-tuple-element.159), channel_id=1, source_target_pairs={{1,0},{2,1},{3,2},{4,3},{5,4},{6,5},{7,6},{8,7},{9,8},{10,9},{11,1... | collective-permute-start | bytes 3080 | tf_op jit(solution)/shard_map/ppermute | solution.py:28
  256.4 4.2 %collective-permute-start.19 = (f32[256,1]{0,1:T(1,128)S(1)}, f32[256,1]{0,1:T(1,128)S(1)}, u32[]{:S(2)}, u32[]{:S(2)}) collective-permute-start(f32[256,1]{0,1:T(1,128)S(1)} %get-tuple-element.160), channel_id=1, source_target_pairs={{0,1},{1,2},{2,3},{3,4},{4,5},{5,6},{6,7},{7,8},{8,9},{9,10},{10,1... | collective-permute-start | bytes 3080 | tf_op jit(solution)/shard_map/ppermute | solution.py:27
  315.3 14.1 %copy-start.7 = (f32[256,512]{0,1:T(8,128)S(1)}, f32[256,512]{0,1:T(8,128)}, u32[]{:S(2)}) copy-start(f32[256,512]{0,1:T(8,128)} %get-tuple-element.52) | copy-start | bytes 1572868
  315.3 14.1 %copy-start.10 = (f32[256,512]{0,1:T(8,128)S(1)}, f32[256,512]{0,1:T(8,128)}, u32[]{:S(2)}) copy-start(f32[256,512]{0,1:T(8,128)} %get-tuple-element.53) | copy-start | bytes 1572868
  315.3 14.1 %copy-start.12 = (f32[256,512]{0,1:T(8,128)S(1)}, f32[256,512]{0,1:T(8,128)}, u32[]{:S(2)}) copy-start(f32[256,512]{0,1:T(8,128)} %get-tuple-element.54) | copy-start | bytes 1572868
  315.3 14.1 %copy-start.14 = (f32[256,512]{0,1:T(8,128)S(1)}, f32[256,512]{0,1:T(8,128)}, u32[]{:S(2)}) copy-start(f32[256,512]{0,1:T(8,128)} %get-tuple-element.55) | copy-start | bytes 1572868
  316.9 12.4 %collective-permute-start.20 = (f32[1,512]{0,1:T(8,128)S(1)}, f32[1,512]{0,1:T(8,128)S(1)}, u32[]{:S(2)}, u32[]{:S(2)}) collective-permute-start(f32[1,512]{0,1:T(8,128)S(1)} %get-tuple-element.158), channel_id=1, source_target_pairs={{32,0},{64,32},{96,64},{33,1},{65,33},{97,65},{34,2},{66,34},{98,6... | collective-permute-start | bytes 6152 | tf_op jit(solution)/shard_map/ppermute | solution.py:28
  318.2 11.1 %collective-permute-start.21 = (f32[1,512]{0,1:T(8,128)S(1)}, f32[1,512]{0,1:T(8,128)S(1)}, u32[]{:S(2)}, u32[]{:S(2)}) collective-permute-start(f32[1,512]{0,1:T(8,128)S(1)} %get-tuple-element.157), channel_id=1, source_target_pairs={{0,32},{32,64},{64,96},{1,33},{33,65},{65,97},{2,34},{34,66},{66,9... | collective-permute-start | bytes 6152 | tf_op jit(solution)/shard_map/ppermute | solution.py:27
  322.2 6.4 %collective-permute-start.22 = (f32[256,1]{0,1:T(1,128)S(1)}, f32[256,1]{0,1:T(1,128)S(1)}, u32[]{:S(2)}, u32[]{:S(2)}) collective-permute-start(f32[256,1]{0,1:T(1,128)S(1)} %get-tuple-element.155), channel_id=1, source_target_pairs={{1,0},{2,1},{3,2},{4,3},{5,4},{6,5},{7,6},{8,7},{9,8},{10,9},{11,1... | collective-permute-start | bytes 3080 | tf_op jit(solution)/shard_map/ppermute | solution.py:28
  325.1 4.2 %collective-permute-start.23 = (f32[256,1]{0,1:T(1,128)S(1)}, f32[256,1]{0,1:T(1,128)S(1)}, u32[]{:S(2)}, u32[]{:S(2)}) collective-permute-start(f32[256,1]{0,1:T(1,128)S(1)} %get-tuple-element.156), channel_id=1, source_target_pairs={{0,1},{1,2},{2,3},{3,4},{4,5},{5,6},{6,7},{7,8},{8,9},{9,10},{10,1... | collective-permute-start | bytes 3080 | tf_op jit(solution)/shard_map/ppermute | solution.py:27
  340.5 44.6 %copy-start.5 = (f32[256,512]{0,1:T(8,128)S(1)}, f32[256,512]{0,1:T(8,128)}, u32[]{:S(2)}) copy-start(f32[256,512]{0,1:T(8,128)} %copy-done.4) | copy-start | bytes 1572868
  340.5 44.6 %copy-start.19 = (f32[256,512]{0,1:T(8,128)S(1)}, f32[256,512]{0,1:T(8,128)}, u32[]{:S(2)}) copy-start(f32[256,512]{0,1:T(8,128)} %copy-done.17) | copy-start | bytes 1572868
  (16 other events, 31.0 us)
